TPU v7x, 256 devices: a whole 4x4x8 slice. The times are simulated.
256 devices in a mesh: ctx: 32 (over y, x, core), batch: 8 (over z).
Axes of the slice: x: 4, y: 4, z: 8, core: 2. Of those that a mesh axis runs over, the one named last changes fastest.
Arguments:
- queries: bfloat16 [98304, 6144], P(('batch', 'ctx')), parts along dimension 0, may hold values from -8 to 8
- keys: bfloat16 [98304, 384], P(('batch', 'ctx')), parts along dimension 0, may hold values from -8 to 8
- values: bfloat16 [98304, 256], P(('batch', 'ctx')), parts along dimension 0, may hold values from -15 to 15
- selected: int32 [1536, 2, 16], P(('batch', 'ctx')), parts along dimension 0, may hold values from -1 to 191, as said below
Outputs:
- attended: bfloat16 [98304, 4096], P(('batch', 'ctx')), parts along dimension 0
There are 8 independent parts, one for each index of `batch`. A program takes and returns all parts, laid end to end along the dimension named above; each array names one. Nothing has to cross between parts.
Inputs may be any that keep to these rules, and one draw needn't show every extreme that they name: `selected`: row b, group g lists distinct blocks c <= b in any order, -1 in the unused slots; blocks 0, b and b - 1 are always listed.
All inputs are finite; a program needn't handle non-finite values.
Results may differ from a plain program's by a relative error of at most 0.0048.
Values may be sent and summed in bfloat16 or wider, within the bound.
A program may use at most 128 MiB of HBM per device.

v0:
```python
import math

import jax
import jax.numpy as jnp
from jax import lax
from jax.sharding import PartitionSpec as P

D_HEAD = 192
D_VALUE = 128
BLOCK = 64


def attend(qblock, near_keys, near_values, chosen, block_index):
    groups, slot_count, block_len, head_dim = near_keys.shape
    value_dim = near_values.shape[3]
    key_rows = near_keys.reshape(groups, slot_count * block_len, head_dim)
    value_rows = near_values.reshape(groups, slot_count * block_len, value_dim)
    scores = jnp.einsum("qghd,gkd->gqhk", qblock, key_rows, preferred_element_type=jnp.float32) * (
        1.0 / math.sqrt(head_dim)
    )
    offsets = jnp.arange(block_len, dtype=jnp.int32)
    key_pos = (jnp.maximum(chosen, 0)[:, :, None] * block_len + offsets[None, None, :]).reshape(
        groups, -1
    )
    listed = jnp.broadcast_to((chosen >= 0)[:, :, None], (groups, slot_count, block_len)).reshape(
        groups, -1
    )
    query_pos = block_index * block_len + offsets
    allowed = listed[:, None, :] & (key_pos[:, None, :] <= query_pos[None, :, None])
    allowed = allowed[:, :, None, :]
    masked = jnp.where(allowed, scores, jnp.float32(-1e30))
    row_max = jnp.max(masked, axis=-1, keepdims=True)
    exp_terms = jnp.where(allowed, jnp.exp(masked - row_max), jnp.float32(0.0))
    row_sum = jnp.sum(exp_terms, axis=-1, keepdims=True)
    weights = (exp_terms / row_sum).astype(jnp.bfloat16)
    result = jnp.einsum("gqhk,gkd->qghd", weights, value_rows, preferred_element_type=jnp.float32)
    return result.astype(jnp.bfloat16).reshape(block_len, -1)


def per_device(queries, keys, values, selected):
    my_index = lax.axis_index("ctx")
    tok_rows = queries.shape[0]
    groups = keys.shape[1] // D_HEAD
    heads_per = queries.shape[1] // (groups * D_HEAD)
    per_dev = tok_rows // BLOCK
    key_part = keys.reshape(per_dev, BLOCK, groups, D_HEAD)
    value_part = values.reshape(per_dev, BLOCK, groups, D_VALUE)
    kv_table = jnp.concatenate([key_part, value_part], axis=3).transpose(0, 2, 1, 3)
    block_ids = jnp.maximum(selected, 0)
    group_ids = jnp.arange(groups, dtype=jnp.int32)[None, :, None]
    first_block = my_index * per_dev
    whole = lax.all_gather(kv_table, "ctx", axis=0, tiled=True)
    chosen = whole[block_ids, group_ids]
    query_blocks = queries.reshape(per_dev, BLOCK, groups, heads_per, D_HEAD)

    def per_block(inputs):
        local_block, qblock, near, picks = inputs
        return attend(
            qblock, near[..., :D_HEAD], near[..., D_HEAD:], picks, first_block + local_block
        )

    result = lax.map(
        per_block, (jnp.arange(per_dev, dtype=jnp.int32), query_blocks, chosen, selected)
    )
    return result.reshape(tok_rows, -1)


def solution(mesh):
    return jax.shard_map(
        per_device,
        mesh=mesh,
        in_specs=(
            P(("batch", "ctx"), None),
            P(("batch", "ctx"), None),
            P(("batch", "ctx"), None),
            P(("batch", "ctx"), None, None),
        ),
        out_specs=P(("batch", "ctx"), None),
        check_vma=False,
    )
```

profile of v0, /device:TPU:1, one launch (start us, length us, event | category | flops | bytes accessed | tf_op | source)
XLA Modules:
  0.0 261.5 jit_solution(4503806383927168346)
XLA Ops:
  6.5 1.0 reshape.67
  7.5 1.2 reshape.66
  8.7 0.9 maximum_bitcast_fusion
  9.6 0.9 copy.20
  10.6 0.7 bitcast_or_fusion
  11.4 11.1 %reshape.68 = bf16[6,64,2,16,192]{4,3,2,1,0:T(8,128)(2,1)} reshape(bf16[384,6144]{1,0:T(8,128)(2,1)} %param.6) | data formatting | bytes 9437184 | tf_op jit(solution)/shard_map/reshape | solution.py:54
  22.5 74.8 %all-gather.2.cloned.1.call-done = bf16[192,2,64,320]{3,2,1,0:T(8,128)(2,1)} async-done(((bf16[6,2,64,320]{3,2,1,0:T(8,128)(2,1)}), bf16[192,2,64,320]{3,2,1,0:T(8,128)(2,1)}) %all-gather.2.cloned.1.call-update) | async-done | bytes 15728656 | tf_op jit(solution)/shard_map/all_gather | solution.py:52
  97.3 17.3 %gather_fusion = bf16[192,64,320]{2,1,0:T(8,128)(2,1)} fusion(bf16[192,2,64,320]{3,2,1,0:T(8,128)(2,1)} %all-gather.2.cloned.1.call-done, s32[192]{0:T(256)S(1)} %reshape.70), kind=kCustom, calls=%fused_computation | custom fusion | bytes 15730176 | tf_op jit(solution)/shard_map/gather | solution.py:53
  114.6 140.1 %while.10 = (s32[]{:T(128)}, bf16[6,64,4096]{2,1,0:T(8,128)(2,1)}, bf16[6,2,16,64,320]{4,3,2,1,0:T(8,128)(2,1)}, s32[6,2,16]{2,1,0:T(2,128)}, s32[6]{0:T(128)S(1...) while((s32[]{:T(128)}, bf16[6,64,4096]{2,1,0:T(8,128)(2,1)}, ...), condition=%wide.region_3.4_spmd, body=%wide.region_0.3_spmd.sunk | while | flops 1361579136 | bytes 53568736 | solution.py:62
  116.0 0.7 compare_bitcast_fusion.2
  117.9 1.6 dynamic-slice_bitcast_fusion.2
  119.8 2.5 fusion.28
  122.3 5.7 %fusion.29 = (f32[2,64,16]{2,1,0:T(8,128)S(1)}, f32[2,64,16,1024]{3,2,1,0:T(8,128)}) fusion(f32[2,64,16,1024]{3,2,1,0:T(8,128)S(1)} %fusion.28, pred[2,64,1024]{2,1,0:T(8,128)(4,1)S(1)} %compare_and_fusion.2), kind=kOutput, calls=%fused_computation.28.clone.1 | output fusion | flops 14681087 | bytes 16916480 | tf_op jit(solution)/shard_map/while/body/eval_jaxpr/sub | solution.py:33
  128.0 4.0 %divide_convert_fusion.2 = bf16[2,64,16,1024]{3,2,1,0:T(8,128)(2,1)S(1)} fusion(f32[2,64,16,1024]{3,2,1,0:T(8,128)} %get-tuple-element.125, f32[2,64,16]{2,1,0:T(8,128)S(1)} %get-tuple-element.126), kind=kLoop, calls=%fused_computation.2.clone.1 | loop fusion | flops 4194304 | bytes 12591104 | tf_op jit(solution)/shard_map/while/body/eval_jaxpr/convert_element_type | solution.py:35
  132.0 4.5 %fusion.30 = bf16[64,2,16,128]{3,0,2,1:T(8,128)(2,1)S(1)} fusion(bf16[2,1024,128,1]{2,1,3,0:T(8,128)(2,1)S(1)} %bitcast.56, bf16[2,64,16,1024]{3,2,1,0:T(8,128)(2,1)S(1)} %divide_convert_fusion.2), kind=kOutput, calls=%fused_computation.13.clone.1 | convolution fusion | flops 537133056 | bytes 5242880 | tf_op jit(solution)/shard_map/while/body/eval_jaxpr/gqhk,gkd->qghd/dot_general | solution.py:36
  137.1 0.8 constant_dynamic-update-slice_fusion.2
  139.3 0.7 compare_bitcast_fusion.2
  141.2 1.6 dynamic-slice_bitcast_fusion.2
  143.1 2.5 fusion.28
  145.7 5.7 %fusion.29 = (f32[2,64,16]{2,1,0:T(8,128)S(1)}, f32[2,64,16,1024]{3,2,1,0:T(8,128)}) fusion(f32[2,64,16,1024]{3,2,1,0:T(8,128)S(1)} %fusion.28, pred[2,64,1024]{2,1,0:T(8,128)(4,1)S(1)} %compare_and_fusion.2), kind=kOutput, calls=%fused_computation.28.clone.1 | output fusion | flops 14681087 | bytes 16916480 | tf_op jit(solution)/shard_map/while/body/eval_jaxpr/sub | solution.py:33
  151.3 4.0 %divide_convert_fusion.2 = bf16[2,64,16,1024]{3,2,1,0:T(8,128)(2,1)S(1)} fusion(f32[2,64,16,1024]{3,2,1,0:T(8,128)} %get-tuple-element.125, f32[2,64,16]{2,1,0:T(8,128)S(1)} %get-tuple-element.126), kind=kLoop, calls=%fused_computation.2.clone.1 | loop fusion | flops 4194304 | bytes 12591104 | tf_op jit(solution)/shard_map/while/body/eval_jaxpr/convert_element_type | solution.py:35
  155.4 4.5 %fusion.30 = bf16[64,2,16,128]{3,0,2,1:T(8,128)(2,1)S(1)} fusion(bf16[2,1024,128,1]{2,1,3,0:T(8,128)(2,1)S(1)} %bitcast.56, bf16[2,64,16,1024]{3,2,1,0:T(8,128)(2,1)S(1)} %divide_convert_fusion.2), kind=kOutput, calls=%fused_computation.13.clone.1 | convolution fusion | flops 537133056 | bytes 5242880 | tf_op jit(solution)/shard_map/while/body/eval_jaxpr/gqhk,gkd->qghd/dot_general | solution.py:36
  160.4 0.8 constant_dynamic-update-slice_fusion.2
  162.7 0.7 compare_bitcast_fusion.2
  164.6 1.6 dynamic-slice_bitcast_fusion.2
  166.5 2.5 fusion.28
  169.0 5.7 %fusion.29 = (f32[2,64,16]{2,1,0:T(8,128)S(1)}, f32[2,64,16,1024]{3,2,1,0:T(8,128)}) fusion(f32[2,64,16,1024]{3,2,1,0:T(8,128)S(1)} %fusion.28, pred[2,64,1024]{2,1,0:T(8,128)(4,1)S(1)} %compare_and_fusion.2), kind=kOutput, calls=%fused_computation.28.clone.1 | output fusion | flops 14681087 | bytes 16916480 | tf_op jit(solution)/shard_map/while/body/eval_jaxpr/sub | solution.py:33
  174.7 4.0 %divide_convert_fusion.2 = bf16[2,64,16,1024]{3,2,1,0:T(8,128)(2,1)S(1)} fusion(f32[2,64,16,1024]{3,2,1,0:T(8,128)} %get-tuple-element.125, f32[2,64,16]{2,1,0:T(8,128)S(1)} %get-tuple-element.126), kind=kLoop, calls=%fused_computation.2.clone.1 | loop fusion | flops 4194304 | bytes 12591104 | tf_op jit(solution)/shard_map/while/body/eval_jaxpr/convert_element_type | solution.py:35
  178.7 4.5 %fusion.30 = bf16[64,2,16,128]{3,0,2,1:T(8,128)(2,1)S(1)} fusion(bf16[2,1024,128,1]{2,1,3,0:T(8,128)(2,1)S(1)} %bitcast.56, bf16[2,64,16,1024]{3,2,1,0:T(8,128)(2,1)S(1)} %divide_convert_fusion.2), kind=kOutput, calls=%fused_computation.13.clone.1 | convolution fusion | flops 537133056 | bytes 5242880 | tf_op jit(solution)/shard_map/while/body/eval_jaxpr/gqhk,gkd->qghd/dot_general | solution.py:36
  183.8 0.8 constant_dynamic-update-slice_fusion.2
  187.9 1.6 dynamic-slice_bitcast_fusion.2
  189.8 2.5 fusion.28
  192.4 5.7 %fusion.29 = (f32[2,64,16]{2,1,0:T(8,128)S(1)}, f32[2,64,16,1024]{3,2,1,0:T(8,128)}) fusion(f32[2,64,16,1024]{3,2,1,0:T(8,128)S(1)} %fusion.28, pred[2,64,1024]{2,1,0:T(8,128)(4,1)S(1)} %compare_and_fusion.2), kind=kOutput, calls=%fused_computation.28.clone.1 | output fusion | flops 14681087 | bytes 16916480 | tf_op jit(solution)/shard_map/while/body/eval_jaxpr/sub | solution.py:33
  198.0 4.0 %divide_convert_fusion.2 = bf16[2,64,16,1024]{3,2,1,0:T(8,128)(2,1)S(1)} fusion(f32[2,64,16,1024]{3,2,1,0:T(8,128)} %get-tuple-element.125, f32[2,64,16]{2,1,0:T(8,128)S(1)} %get-tuple-element.126), kind=kLoop, calls=%fused_computation.2.clone.1 | loop fusion | flops 4194304 | bytes 12591104 | tf_op jit(solution)/shard_map/while/body/eval_jaxpr/convert_element_type | solution.py:35
  202.0 4.5 %fusion.30 = bf16[64,2,16,128]{3,0,2,1:T(8,128)(2,1)S(1)} fusion(bf16[2,1024,128,1]{2,1,3,0:T(8,128)(2,1)S(1)} %bitcast.56, bf16[2,64,16,1024]{3,2,1,0:T(8,128)(2,1)S(1)} %divide_convert_fusion.2), kind=kOutput, calls=%fused_computation.13.clone.1 | convolution fusion | flops 537133056 | bytes 5242880 | tf_op jit(solution)/shard_map/while/body/eval_jaxpr/gqhk,gkd->qghd/dot_general | solution.py:36
  207.1 0.8 constant_dynamic-update-slice_fusion.2
  211.3 1.6 dynamic-slice_bitcast_fusion.2
  213.2 2.5 fusion.28
  215.7 5.7 %fusion.29 = (f32[2,64,16]{2,1,0:T(8,128)S(1)}, f32[2,64,16,1024]{3,2,1,0:T(8,128)}) fusion(f32[2,64,16,1024]{3,2,1,0:T(8,128)S(1)} %fusion.28, pred[2,64,1024]{2,1,0:T(8,128)(4,1)S(1)} %compare_and_fusion.2), kind=kOutput, calls=%fused_computation.28.clone.1 | output fusion | flops 14681087 | bytes 16916480 | tf_op jit(solution)/shard_map/while/body/eval_jaxpr/sub | solution.py:33
  221.4 4.0 %divide_convert_fusion.2 = bf16[2,64,16,1024]{3,2,1,0:T(8,128)(2,1)S(1)} fusion(f32[2,64,16,1024]{3,2,1,0:T(8,128)} %get-tuple-element.125, f32[2,64,16]{2,1,0:T(8,128)S(1)} %get-tuple-element.126), kind=kLoop, calls=%fused_computation.2.clone.1 | loop fusion | flops 4194304 | bytes 12591104 | tf_op jit(solution)/shard_map/while/body/eval_jaxpr/convert_element_type | solution.py:35
  225.4 4.5 %fusion.30 = bf16[64,2,16,128]{3,0,2,1:T(8,128)(2,1)S(1)} fusion(bf16[2,1024,128,1]{2,1,3,0:T(8,128)(2,1)S(1)} %bitcast.56, bf16[2,64,16,1024]{3,2,1,0:T(8,128)(2,1)S(1)} %divide_convert_fusion.2), kind=kOutput, calls=%fused_computation.13.clone.1 | convolution fusion | flops 537133056 | bytes 5242880 | tf_op jit(solution)/shard_map/while/body/eval_jaxpr/gqhk,gkd->qghd/dot_general | solution.py:36
  230.5 0.8 constant_dynamic-update-slice_fusion.2
  234.6 1.6 dynamic-slice_bitcast_fusion.2
  236.5 2.5 fusion.28
  239.0 5.7 %fusion.29 = (f32[2,64,16]{2,1,0:T(8,128)S(1)}, f32[2,64,16,1024]{3,2,1,0:T(8,128)}) fusion(f32[2,64,16,1024]{3,2,1,0:T(8,128)S(1)} %fusion.28, pred[2,64,1024]{2,1,0:T(8,128)(4,1)S(1)} %compare_and_fusion.2), kind=kOutput, calls=%fused_computation.28.clone.1 | output fusion | flops 14681087 | bytes 16916480 | tf_op jit(solution)/shard_map/while/body/eval_jaxpr/sub | solution.py:33
  244.7 4.0 %divide_convert_fusion.2 = bf16[2,64,16,1024]{3,2,1,0:T(8,128)(2,1)S(1)} fusion(f32[2,64,16,1024]{3,2,1,0:T(8,128)} %get-tuple-element.125, f32[2,64,16]{2,1,0:T(8,128)S(1)} %get-tuple-element.126), kind=kLoop, calls=%fused_computation.2.clone.1 | loop fusion | flops 4194304 | bytes 12591104 | tf_op jit(solution)/shard_map/while/body/eval_jaxpr/convert_element_type | solution.py:35
  248.7 4.5 %fusion.30 = bf16[64,2,16,128]{3,0,2,1:T(8,128)(2,1)S(1)} fusion(bf16[2,1024,128,1]{2,1,3,0:T(8,128)(2,1)S(1)} %bitcast.56, bf16[2,64,16,1024]{3,2,1,0:T(8,128)(2,1)S(1)} %divide_convert_fusion.2), kind=kOutput, calls=%fused_computation.13.clone.1 | convolution fusion | flops 537133056 | bytes 5242880 | tf_op jit(solution)/shard_map/while/body/eval_jaxpr/gqhk,gkd->qghd/dot_general | solution.py:36
  253.8 0.8 constant_dynamic-update-slice_fusion.2
  (98 shorter events, 18.8 us)
Async XLA Ops:
  6.5 90.8 %all-gather.2.cloned.1.call-start = ((), (), s32[]{:S(2)}) async-start(), calls=%async_computation | async-start | bytes 19464192 | tf_op jit(solution)/shard_map/all_gather | solution.py:52
Sparse Core Ops, SparseCore 0:
  10.7 86.5 all-gather.1
where the time goes:
time: 263 us; the launch traced here: 262 us
  waiting for transfers between devices  74.8 us (28%)
  other arithmetic  68.9 us (26%)
  local copies, waits for them, and re-layouts  57.6 us (22%)
  matrix products  42.2 us (16%)
  between operations  13.4 us (5%)
  loops' own time  4.6 us (2%)
    all_gather x1, waiting for transfers between devices, per_device(): whole = lax.all_gather(kv_table, 'ctx', axis=0, tiled=True)  74.8 us
    sub x6, other arithmetic, attend(): exp_terms = jnp.where(allowed, jnp.exp(masked - row_max), jnp.float32(0.0))  34 us
    dot_general x6, matrix products, attend(): jnp.einsum('gqhk,gkd->qghd', weights, value_rows, preferred_element_type=...  27.1 us
    convert_element_type x6, other arithmetic, attend(): weights = (exp_terms / row_sum).astype(jnp.bfloat16)  24.1 us
    gather x1, local copies, waits for them, and re-layouts, per_device(): chosen = whole[block_ids, group_ids]  17.3 us
    dot_general x6, matrix products, attend(): jnp.einsum('qghd,gkd->gqhk', qblock, key_rows, preferred_element_type=jnp...  15.1 us
    reshape x1, local copies, waits for them, and re-layouts, per_device(): query_blocks = queries.reshape(per_dev, BLOCK, groups, heads_per, D_HEAD)  11.1 us
    squeeze x6, local copies, waits for them, and re-layouts, per_device(): lax.map(per_block, (jnp.arange(per_dev, dtype=jnp.int32), query_blocks, c...  9.45 us
  transfers between devices with their start and end apart: 1, of which 1 were waited for; matrix products, arithmetic and copies ran while one was open for 5% of the time, Pallas kernels for 0%

commit v1 on v0

v1 whole, which is shorter than its diff:
```python
import functools
import math

import jax
import jax.numpy as jnp
from jax import lax
from jax.experimental import pallas as pl
from jax.experimental.pallas import tpu as pltpu
from jax.sharding import PartitionSpec as P

D_HEAD = 192
D_VALUE = 128
BLOCK = 64
SIDE = 4
LANES = 128
SHARD = 3
BUNDLE = SIDE * SHARD
PIECES = 24
NEG = -1e30
EMPTY = 2 * 2 * SIDE * SIDE * 3


def copies_of(first, table, send_sem, recv_sem):
    me = lax.axis_index("ctx")
    core = lax.rem(me, 2)
    chip = lax.div(me, 2)
    y = lax.div(chip, SIDE)
    x = lax.rem(chip, SIDE)
    xp, xm, x2 = (lax.rem(x + d, SIDE) for d in (1, 3, 2))
    yp, ym, y2 = (lax.rem(y + d, SIDE) for d in (1, 3, 2))

    def device(row, column):
        return (row * SIDE + column) * 2 + core

    right, left = device(y, xp), device(y, xm)
    down, up = device(yp, x), device(ym, x)
    partner = chip * 2 + (1 - core)

    def row_a(row, column):
        return (core * SIDE * SIDE + row * SIDE + column) * SHARD

    def row_b(column, row):
        return ((2 + core) * SIDE * SIDE + column * SIDE + row) * SHARD

    rest, half_bundle = SHARD - first, BUNDLE // 2
    plan = [
        (row_a(y, x), SHARD, right),
        (row_a(y, x), SHARD, left),
        (row_b(x, y), SHARD, down),
        (row_b(x, y), SHARD, up),
        (row_a(y, xm), first, right),
        (row_a(y, xp) + first, rest, left),
        (row_b(x, ym), rest, down),
        (row_b(x, yp) + rest, first, up),
        (row_a(y, 0), BUNDLE, down),
        (row_a(y, 0), BUNDLE, up),
        (row_b(x, 0), BUNDLE, right),
        (row_b(x, 0), BUNDLE, left),
        (row_a(y, 0), BUNDLE, partner),
        (row_b(x, 0), BUNDLE, partner),
        (row_a(ym, 0), half_bundle, down),
        (row_a(yp, 0) + half_bundle, half_bundle, up),
        (row_b(xm, 0), half_bundle, right),
        (row_b(xp, 0) + half_bundle, half_bundle, left),
        (row_a(ym, 0), BUNDLE, partner),
        (row_a(yp, 0), BUNDLE, partner),
        (row_b(xm, 0), BUNDLE, partner),
        (row_b(xp, 0), BUNDLE, partner),
        (row_a(y2, 0), BUNDLE, partner),
        (row_b(x2, 0), BUNDLE, partner),
    ]
    made = []
    for n, (row, count, peer) in enumerate(plan):
        place = table.at[pl.ds(row, count)]
        made.append(
            pltpu.make_async_remote_copy(
                src_ref=place,
                dst_ref=place,
                send_sem=send_sem.at[n],
                recv_sem=recv_sem.at[n],
                device_id={"ctx": peer},
                device_id_type=pl.DeviceIdType.MESH,
            )
        )
    peers = (right, left, down, up, partner)
    own = (row_a(y, x), row_b(x, y))
    return made, peers, own


def places_of(selected, first_block):
    own = first_block + lax.broadcasted_iota(jnp.int32, selected.shape, 0)
    spot = lax.broadcasted_iota(jnp.int32, selected.shape, 2)
    head = jnp.broadcast_to(selected[:, :, 0:1], selected.shape)
    listed = jnp.where(spot == 0, own, jnp.where(selected == own, head, selected))
    device = (listed * 10923) >> 16
    within = listed - 6 * device
    chip, core = device >> 1, device & 1
    turned = (chip & (SIDE - 1)) * SIDE + (chip >> 2)
    late = within >= SHARD
    place = jnp.where(late, turned, chip)
    within = jnp.where(late, within - SHARD, within)
    slot = (jnp.where(late, 2, 0) + core) * (SIDE * SIDE * SHARD) + place * SHARD + within
    used = listed >= 0
    return jnp.where(used, slot, EMPTY), jnp.where(used, 0, 1)


def kernel(
    heads_per,
    sel_ref,
    q_hbm,
    k_hbm,
    v_hbm,
    out_hbm,
    t0,
    t1,
    t2,
    t3,
    t4,
    q_stage,
    q_rows,
    weights,
    k_near,
    v_near,
    counts,
    place_stage,
    count_stage,
    place_ref,
    count_ref,
    out_stage,
    send_sem,
    recv_sem,
    load_sem,
    q_sem,
    place_sem,
    out_sem,
):
    tables = (t0, t1, t2, t3, t4)
    blocks = q_stage.shape[0]
    slots = sel_ref.shape[2]
    first_block = lax.axis_index("ctx") * blocks
    all_copies = []
    for j, table in enumerate(tables):
        made, peers, own = copies_of(1 + j % 2, table, send_sem.at[j], recv_sem.at[j])
        all_copies.append(made)

    loads = []
    for j, table in enumerate(tables):
        source = k_hbm if j < 3 else v_hbm
        column = (j if j < 3 else j - 3) * LANES
        for half in range(2):
            loads.append(
                pltpu.make_async_copy(
                    source.at[pl.ds(half * SHARD, SHARD), :, pl.ds(column, LANES)],
                    table.at[pl.ds(own[half], SHARD)],
                    load_sem.at[j * 2 + half],
                )
            )
    for load in loads:
        load.start()
    q_loads = [
        pltpu.make_async_copy(q_hbm.at[pl.ds(b * BLOCK, BLOCK)], q_stage.at[b], q_sem.at[b])
        for b in range(blocks)
    ]
    for load in q_loads:
        load.start()

    barrier = pltpu.get_barrier_semaphore()
    for peer in peers:
        pl.semaphore_signal(
            barrier, inc=1, device_id={"ctx": peer}, device_id_type=pl.DeviceIdType.MESH
        )
    pl.semaphore_wait(barrier, len(peers))

    def go(j, names):
        for n in names:
            all_copies[j][n].start()

    def arrived(j, names):
        for n in names:
            all_copies[j][n].wait_recv()

    def step1(j):
        arrived(j, range(0, 4))
        go(j, range(4, 8))

    def step2(j):
        arrived(j, range(4, 8))
        go(j, range(8, 14))

    def step3(j):
        arrived(j, range(8, 12))
        go(j, range(14, 22))

    def step4(j):
        arrived(j, range(14, 18))
        go(j, range(22, 24))

    def step5(j):
        arrived(j, (12, 13, 18, 19, 20, 21, 22, 23))
        if j < 3:
            tables[j][EMPTY] = jnp.broadcast_to(tables[j][0, 0:1, :], (BLOCK, LANES))
        else:
            tables[j][EMPTY] = jnp.zeros((BLOCK, LANES), jnp.bfloat16)

    lane = lax.broadcasted_iota(jnp.int32, (BLOCK, 2 * LANES), 1)

    def prepare(b):
        q_loads[b].wait()
        for head in range(2 * heads_per):
            group = head // heads_per
            start = head * D_HEAD
            aligned = start // LANES * LANES
            window = q_stage[b, :, aligned : aligned + 2 * LANES].astype(jnp.float32)
            shift = group * 64 - (start - aligned)
            if shift:
                window = pltpu.roll(window, shift % (2 * LANES), 1)
            keep = (lane >= 64) if group else (lane < D_HEAD)
            window = jnp.where(keep, window, 0.0).astype(jnp.bfloat16)
            at = (head - group * heads_per) * BLOCK
            q_rows[group * blocks + b, at : at + BLOCK, :] = window

    scale = math.log2(math.e) / math.sqrt(D_HEAD)
    chunk = heads_per // 2 * BLOCK
    causal = lax.broadcasted_iota(jnp.int32, (BLOCK, LANES), 1)
    causal = (causal >= BLOCK) | (causal <= lax.broadcasted_iota(jnp.int32, (BLOCK, LANES), 0))

    def score(b, group):
        low, high = tables[group], tables[group + 1]
        for i in range(slots):
            place = place_ref[b, group, i]
            at = i * BLOCK
            k_near[at : at + BLOCK, 0:LANES] = low[place]
            k_near[at : at + BLOCK, LANES : 2 * LANES] = high[place]
        pair = group * blocks + b

        def part(half, _):
            rows = pl.ds(pl.multiple_of(half * chunk, chunk), chunk)
            s = lax.dot_general(
                q_rows[pair, rows, :],
                k_near[...],
                (((1,), (1,)), ((), ())),
                preferred_element_type=jnp.float32,
            )
            edge = s[:, 0:LANES].reshape(heads_per // 2, BLOCK, LANES)
            edge = jnp.where(causal[None], edge, NEG).reshape(chunk, LANES)
            s = jnp.concatenate([edge, s[:, LANES:]], axis=1)
            top = jnp.max(s, axis=1, keepdims=True)
            weights[pair, rows, :] = jnp.exp2((s - top) * scale).astype(jnp.bfloat16)
            return 0

        lax.fori_loop(0, 2, part, 0)

    def attend(b, group):
        table = tables[3 + group]
        for i in range(slots):
            at = i * BLOCK
            v_near[at : at + BLOCK, 0:LANES] = table[place_ref[b, group, i]]
            v_near[at : at + BLOCK, LANES : 2 * LANES] = counts[count_ref[b, group, i]]
        pair = group * blocks + b
        for half in range(2):
            o = jnp.dot(
                weights[pair, half * chunk : (half + 1) * chunk, :],
                v_near[...],
                preferred_element_type=jnp.float32,
            )
            o = (o[:, 0:LANES] / o[:, LANES:]).astype(jnp.bfloat16)
            for h in range(heads_per // 2):
                column = (group * heads_per + half * (heads_per // 2) + h) * D_VALUE
                out_stage[b, :, column : column + D_VALUE] = o[h * BLOCK : (h + 1) * BLOCK]

    def score_blocks(group, low, high):
        lax.fori_loop(low, high, lambda b, c: (score(b, group), c)[1], 0)

    def attend_blocks(group, low, high):
        lax.fori_loop(low, high, lambda b, c: (attend(b, group), c)[1], 0)

    width = heads_per * D_VALUE
    stores = {}

    def put(group, b):
        columns = pl.ds(group * width, width)
        stores[group, b] = pltpu.make_async_copy(
            out_stage.at[b, :, columns],
            out_hbm.at[pl.ds(b * BLOCK, BLOCK), columns],
            out_sem.at[group * blocks + b],
        )
        stores[group, b].start()

    for j in range(5):
        loads[2 * j].wait()
        loads[2 * j + 1].wait()
        go(j, range(0, 4))
    place_stage[...], count_stage[...] = places_of(sel_ref[...], first_block)
    place_copies = [
        pltpu.make_async_copy(place_stage, place_ref, place_sem.at[0]),
        pltpu.make_async_copy(count_stage, count_ref, place_sem.at[1]),
    ]
    counts[0] = jnp.ones((BLOCK, LANES), jnp.bfloat16)
    counts[1] = jnp.zeros((BLOCK, LANES), jnp.bfloat16)
    for j in range(5):
        prepare(j)
        step1(j)
    step2(0)
    step2(1)
    for copy in place_copies:
        copy.start()
    prepare(5)
    for copy in place_copies:
        copy.wait()
    step3(0)
    step2(2)
    step3(1)
    step2(3)
    step4(0)
    step3(2)
    step2(4)
    step4(1)
    step5(0)
    step5(1)
    score_blocks(0, 0, 2)
    step3(3)
    score_blocks(0, 2, 4)
    step4(2)
    score_blocks(0, 4, 6)
    step3(4)
    step5(2)
    score_blocks(1, 0, 3)
    step4(3)
    score_blocks(1, 3, 6)
    step5(3)
    attend_blocks(0, 0, 3)
    step4(4)
    attend_blocks(0, 3, 6)
    for b in range(blocks):
        put(0, b)
    step5(4)
    attend_blocks(1, 0, 6)
    for b in range(blocks):
        put(1, b)
    for made in all_copies:
        for copy in made:
            copy.wait_send()
    for store in stores.values():
        store.wait()


def per_device(queries, keys, values, selected):
    rows = queries.shape[0]
    blocks = rows // BLOCK
    groups = keys.shape[1] // D_HEAD
    heads_per = queries.shape[1] // (groups * D_HEAD)
    entries = blocks * 2 * SIDE * SIDE + 1
    spots = selected.shape[2] * BLOCK
    anywhere = pl.BlockSpec(memory_space=pl.ANY)
    return pl.pallas_call(
        functools.partial(kernel, heads_per),
        out_shape=jax.ShapeDtypeStruct((rows, groups * heads_per * D_VALUE), jnp.bfloat16),
        in_specs=[pl.BlockSpec(memory_space=pltpu.VMEM), anywhere, anywhere, anywhere],
        out_specs=anywhere,
        scratch_shapes=[pltpu.VMEM((entries, BLOCK, LANES), jnp.bfloat16)] * 5
        + [
            pltpu.VMEM((blocks, BLOCK, queries.shape[1]), jnp.bfloat16),
            pltpu.VMEM((groups * blocks, heads_per * BLOCK, 2 * LANES), jnp.bfloat16),
            pltpu.VMEM((groups * blocks, heads_per * BLOCK, spots), jnp.bfloat16),
            pltpu.VMEM((spots, 2 * LANES), jnp.bfloat16),
            pltpu.VMEM((spots, 2 * LANES), jnp.bfloat16),
            pltpu.VMEM((2, BLOCK, LANES), jnp.bfloat16),
            pltpu.VMEM(selected.shape, jnp.int32),
            pltpu.VMEM(selected.shape, jnp.int32),
            pltpu.SMEM(selected.shape, jnp.int32),
            pltpu.SMEM(selected.shape, jnp.int32),
            pltpu.VMEM((blocks, BLOCK, groups * heads_per * D_VALUE), jnp.bfloat16),
            pltpu.SemaphoreType.DMA((5, PIECES)),
            pltpu.SemaphoreType.DMA((5, PIECES)),
            pltpu.SemaphoreType.DMA((10,)),
            pltpu.SemaphoreType.DMA((blocks,)),
            pltpu.SemaphoreType.DMA((2,)),
            pltpu.SemaphoreType.DMA((groups * blocks,)),
        ],
        compiler_params=pltpu.CompilerParams(
            collective_id=0, has_side_effects=True, vmem_limit_bytes=67043328
        ),
        name="gather_attend",
    )(
        selected,
        queries,
        keys.reshape(blocks, BLOCK, keys.shape[1]),
        values.reshape(blocks, BLOCK, values.shape[1]),
    )


def solution(mesh):
    rows = P(("batch", "ctx"), None)
    return jax.shard_map(
        per_device,
        mesh=mesh,
        in_specs=(rows, rows, rows, P(("batch", "ctx"), None, None)),
        out_specs=rows,
        check_vma=False,
    )
```

time: 263 us -> 71.4 us (0.27)
  waiting for transfers between devices: 74.8 us -> 0 us
  other arithmetic: 68.9 us -> 0 us
  Pallas kernels: 0 us -> 67.3 us
  local copies, waits for them, and re-layouts: 57.6 us -> 3.91 us
  matrix products: 42.2 us -> 0 us
  between operations: 13.4 us -> 0.01 us
  loops' own time: 4.6 us -> 0 us
    all_gather x1 -> x0, waiting for transfers between devices: 74.8 us -> none  [per_device(): whole = lax.all_gather(kv_table, 'ctx', axis=0, tiled=True)]
    pallas_call x0 -> x1, Pallas kernels: none -> 67.3 us  [per_device(): pl.pallas_call(functools.partial(kernel, heads_per), out_shape=jax.ShapeD...]
    dot_general x12 -> x0, matrix products: 42.2 us -> none  [the longest x6 27.1 us: attend(): jnp.einsum('gqhk,gkd->qghd', weights, value_rows, preferred_element_type=...]
    sub x6 -> x0, other arithmetic: 34 us -> none  [attend(): exp_terms = jnp.where(allowed, jnp.exp(masked - row_max), jnp.float32(0.0))]
    convert_element_type x6 -> x0, other arithmetic: 24.1 us -> none  [attend(): weights = (exp_terms / row_sum).astype(jnp.bfloat16)]
    gather x1 -> x0, local copies, waits for them, and re-layouts: 17.3 us -> none  [per_device(): chosen = whole[block_ids, group_ids]]
    reshape x3 -> x0, local copies, waits for them, and re-layouts: 13.3 us -> none  [the longest x1 11.1 us: per_device(): query_blocks = queries.reshape(per_dev, BLOCK, groups, heads_per, D_HEAD)]
    squeeze x6 -> x0, local copies, waits for them, and re-layouts: 9.45 us -> none  [per_device(): lax.map(per_block, (jnp.arange(per_dev, dtype=jnp.int32), query_blocks, c...]
  transfers between devices with their start and end apart: 1 -> 0, of which waited for: 1 -> 0; matrix products, arithmetic and copies ran while one was open for 5% -> 0% of each run, Pallas kernels for 0% -> 0%
where the time goes in v1:
time: 71.4 us; the launch traced here: 71.2 us
  Pallas kernels  67.3 us (94%)
  local copies, waits for them, and re-layouts  3.91 us (5%)
    pallas_call x1, Pallas kernels, per_device(): pl.pallas_call(functools.partial(kernel, heads_per), out_shape=jax.ShapeD...  67.3 us
    unnamed x1, local copies, waits for them, and re-layouts  3.91 us

profile of v1, /device:TPU:1, one launch (start us, length us, event | category | flops | bytes accessed | tf_op | source)
XLA Modules:
  0.0 71.2 jit_solution(5871249351393217583)
XLA Ops:
  0.0 67.3 %gather_attend.1 = bf16[384,4096]{1,0:T(8,128)(2,1)} custom-call(s32[6,2,16]{2,1,0:T(2,128)} %sel_ref.1, bf16[384,6144]{1,0:T(8,128)(2,1)} %q_hbm.1, bf16[6,64,384]{2,1,0:T(8,128)(2,1)} %bitcast.2, bf16[6,64,256]{2,1,0:T(8,128)(2,1)} %bitcast.3), custom_call_target="tpu_custom_call" | custom-call | tf_op jit(solution)/shard_map/gather_attend/pallas_call | solution.py:355
  67.3 3.9 %copy.6 = bf16[384,4096]{1,0:T(8,128)(2,1)} copy(bf16[384,4096]{1,0:T(8,128)(2,1)} %gather_attend.1) | data formatting | bytes 6291456

commit v2 on v1

v2 whole, which is shorter than its diff:
```python
import functools
import math

import jax
import jax.numpy as jnp
from jax import lax
from jax.experimental import pallas as pl
from jax.experimental.pallas import tpu as pltpu
from jax.sharding import PartitionSpec as P

D_HEAD = 192
D_VALUE = 128
BLOCK = 64
SIDE = 4
LANES = 128
SHARD = 3
BUNDLE = SIDE * SHARD
PIECES = 24
NEG = -1e30
PLAN = (
    "01", "00", "02", "q0", "03", "11", "10", "04", "12", "q1", "q2", "13", "21", "q3", "20", "q4", "q5", "22", "31",
    "30", "14", "32", "23", "41", "40", "50", "51", "s0", "42", "s1", "24", "s2", "s3", "s4", "s5", "s6", "s7", "s8",
    "33", "52", "s9", "s10", "s11", "s12", "s13", "s14", "s15", "s16", "34", "s17", "s18", "s19", "s20",
    "43", "s21", "s22", "s23", "s24", "53", "v0", "v1", "44", "v2", "v3", "v4", "v5", "54", "v6", "v7", "v8", "v9",
    "v10", "v11",
)
SENT = ("v0", "v1", "v2", "v3", "v10")
EMPTY = 2 * 2 * SIDE * SIDE * 3


def peers_and_rows():
    me = lax.axis_index("ctx")
    core = lax.rem(me, 2)
    chip = lax.div(me, 2)
    y = lax.div(chip, SIDE)
    x = lax.rem(chip, SIDE)
    xp, xm, x2 = (lax.rem(x + d, SIDE) for d in (1, 3, 2))
    yp, ym, y2 = (lax.rem(y + d, SIDE) for d in (1, 3, 2))
    parts = lax.axis_size("batch")
    part = lax.axis_index("batch")

    def device(row, column, on_chip):
        return ((row * SIDE + column) * 2 + on_chip) * parts + part

    def bundle(half, line):
        return ((half * 2 + core) * SIDE + line) * BUNDLE

    peers = dict(
        right=device(y, xp, core),
        left=device(y, xm, core),
        down=device(yp, x, core),
        up=device(ym, x, core),
        partner=device(y, x, 1 - core),
    )
    row = bundle(0, y)
    column = bundle(1, x)
    rows = dict(
        row=row,
        row_own=row + x * SHARD,
        row_left=row + xm * SHARD,
        row_right=row + xp * SHARD,
        row_up=bundle(0, ym),
        row_down=bundle(0, yp),
        row_far=bundle(0, y2),
        column=column,
        column_own=column + y * SHARD,
        column_up=column + ym * SHARD,
        column_down=column + yp * SHARD,
        column_left=bundle(1, xm),
        column_right=bundle(1, xp),
        column_far=bundle(1, x2),
    )
    return peers, rows


def copies_of(first, peers, rows, table, send_sem, recv_sem):
    rest, half = SHARD - first, BUNDLE // 2
    plan = [
        ("row_own", 0, SHARD, "right"),
        ("row_own", 0, SHARD, "left"),
        ("column_own", 0, SHARD, "down"),
        ("column_own", 0, SHARD, "up"),
        ("row_left", 0, first, "right"),
        ("row_right", first, rest, "left"),
        ("column_up", 0, rest, "down"),
        ("column_down", rest, first, "up"),
        ("row", 0, BUNDLE, "down"),
        ("row", 0, BUNDLE, "up"),
        ("column", 0, BUNDLE, "right"),
        ("column", 0, BUNDLE, "left"),
        ("row", 0, BUNDLE, "partner"),
        ("column", 0, BUNDLE, "partner"),
        ("row_up", 0, half, "down"),
        ("row_down", half, half, "up"),
        ("column_left", 0, half, "right"),
        ("column_right", half, half, "left"),
        ("row_up", 0, BUNDLE, "partner"),
        ("row_down", 0, BUNDLE, "partner"),
        ("column_left", 0, BUNDLE, "partner"),
        ("column_right", 0, BUNDLE, "partner"),
        ("row_far", 0, BUNDLE, "partner"),
        ("column_far", 0, BUNDLE, "partner"),
    ]
    made = []
    for n, (name, skip, count, peer) in enumerate(plan):
        place = table.at[pl.ds(rows[name] + skip, count)]
        made.append(
            pltpu.make_async_remote_copy(
                src_ref=place,
                dst_ref=place,
                send_sem=send_sem.at[n],
                recv_sem=recv_sem.at[n],
                device_id=peers[peer],
                device_id_type=pl.DeviceIdType.LOGICAL,
            )
        )
    return made


def places_of(selected, first_block):
    own = first_block + lax.broadcasted_iota(jnp.int32, selected.shape, 0)
    spot = lax.broadcasted_iota(jnp.int32, selected.shape, 2)
    head = jnp.broadcast_to(selected[:, :, 0:1], selected.shape)
    listed = jnp.where(spot == 0, own, jnp.where(selected == own, head, selected))
    device = (listed * 10923) >> 16
    within = listed - 6 * device
    chip, core = device >> 1, device & 1
    turned = (chip & (SIDE - 1)) * SIDE + (chip >> 2)
    late = within >= SHARD
    place = jnp.where(late, turned, chip)
    within = jnp.where(late, within - SHARD, within)
    slot = (jnp.where(late, 2, 0) + core) * (SIDE * SIDE * SHARD) + place * SHARD + within
    used = listed >= 0
    return jnp.where(used, slot, EMPTY), jnp.where(used, 0, 1)


def kernel(
    heads_per,
    sel_ref,
    q_hbm,
    k_hbm,
    v_hbm,
    out_ref,
    t0,
    t1,
    t2,
    t3,
    t4,
    scores_a,
    scores_b,
    weights,
    near_rows,
    counts,
    sel_stage,
    place_stage,
    count_stage,
    place_ref,
    count_ref,
    send_sem,
    recv_sem,
    load_sem,
    q_sem,
    place_sem,
):
    tables = (t0, t1, t2, t3, t4)
    scores = (scores_a, scores_b)
    blocks, groups, slots = sel_ref.shape
    first_block = lax.axis_index("ctx") * blocks
    peers, rows = peers_and_rows()
    barrier = pltpu.get_barrier_semaphore()
    for peer in peers.values():
        pl.semaphore_signal(
            barrier, inc=1, device_id=peer, device_id_type=pl.DeviceIdType.LOGICAL
        )

    own = (rows["row_own"], rows["column_own"])
    loads = []
    for j, table in enumerate(tables):
        source = k_hbm if j < 3 else v_hbm
        column = (j if j < 3 else j - 3) * LANES
        for half in range(2):
            loads.append(
                pltpu.make_async_copy(
                    source.at[pl.ds(half * SHARD, SHARD), :, pl.ds(column, LANES)],
                    table.at[pl.ds(own[half], SHARD)],
                    load_sem.at[j * 2 + half],
                )
            )
    for load in loads:
        load.start()
    near = 2 * LANES
    strips = 2 * heads_per // 4
    q_loads = [
        [
            pltpu.make_async_copy(
                q_hbm.at[pl.ds(b * BLOCK, BLOCK), pl.ds(i * 4 * D_HEAD, 4 * D_HEAD)],
                weights.at[
                    (groups - 1) * blocks + b,
                    pl.ds(i * BLOCK, BLOCK),
                    pl.ds(near, 4 * D_HEAD),
                ],
                q_sem.at[b, i],
            )
            for i in range(strips)
        ]
        for b in range(blocks)
    ]
    for group in q_loads:
        for load in group:
            load.start()

    sel_load = pltpu.make_async_copy(sel_ref, sel_stage, place_sem.at[2])
    sel_load.start()
    pl.semaphore_wait(barrier, len(peers))

    all_copies = {}

    def go(j, names):
        for n in names:
            all_copies[j][n].start()

    def arrived(j, names):
        for n in names:
            all_copies[j][n].wait_recv()

    def step1(j):
        arrived(j, range(0, 4))
        go(j, range(4, 8))

    def step2(j):
        arrived(j, range(4, 8))
        go(j, range(8, 14))

    def step3(j):
        arrived(j, range(8, 12))
        go(j, range(14, 22))

    def step4(j):
        arrived(j, range(14, 18))
        go(j, range(22, 24))

    def step5(j):
        arrived(j, (12, 13, 18, 19, 20, 21, 22, 23))
        if j < 3:
            tables[j][EMPTY] = jnp.broadcast_to(tables[j][0, 0:1, :], (BLOCK, LANES))
        else:
            tables[j][EMPTY] = jnp.zeros((BLOCK, LANES), jnp.bfloat16)

    lane = lax.broadcasted_iota(jnp.int32, (BLOCK, 2 * LANES), 1)

    def prepare(b):
        for load in q_loads[b]:
            load.wait()
        for head in range(2 * heads_per):
            group = head // heads_per
            start = head % 4 * D_HEAD
            aligned = start // LANES * LANES
            strip = head // 4 * BLOCK
            window = weights[
                (groups - 1) * blocks + b,
                strip : strip + BLOCK,
                near + aligned : near + aligned + near,
            ].astype(jnp.float32)
            shift = group * 64 - (start - aligned)
            if shift:
                window = pltpu.roll(window, shift % (2 * LANES), 1)
            keep = (lane >= 64) if group else (lane < D_HEAD)
            window = jnp.where(keep, window, 0.0).astype(jnp.bfloat16)
            at = (head - group * heads_per) * BLOCK
            weights[group * blocks + b, at : at + BLOCK, 0:near] = window

    scale = math.log2(math.e) / math.sqrt(D_HEAD)
    chunk = heads_per // 2 * BLOCK
    causal = lax.broadcasted_iota(jnp.int32, (BLOCK, LANES), 1)
    causal = (causal >= BLOCK) | (causal <= lax.broadcasted_iota(jnp.int32, (BLOCK, LANES), 0))

    half_heads = heads_per // 2

    def near_keys(pair):
        group, b = divmod(pair, blocks)
        low, high = tables[group], tables[group + 1]
        for i in range(slots):
            place = place_ref[b, group, i]
            at = i * BLOCK
            near_rows[pair % 2, at : at + BLOCK, 0:LANES] = low[place]
            near_rows[pair % 2, at : at + BLOCK, LANES : 2 * LANES] = high[place]

    def near_values(pair):
        group, b = divmod(pair, blocks)
        table = tables[3 + group]
        for i in range(slots):
            at = i * BLOCK
            near_rows[pair % 2, at : at + BLOCK, 0:LANES] = table[place_ref[b, group, i]]
            near_rows[pair % 2, at : at + BLOCK, LANES : 2 * LANES] = counts[count_ref[b, group, i]]

    def multiply(unit):
        pair, half = divmod(unit, 2)
        scores[half][...] = lax.dot_general(
            weights[pair, half * chunk : (half + 1) * chunk, 0:near],
            near_rows[pair % 2],
            (((1,), (1,)), ((), ())),
            preferred_element_type=jnp.float32,
        )

    def soften(unit):
        pair, half = divmod(unit, 2)
        s = scores[half][...]
        edge = s[:, 0:LANES].reshape(half_heads, BLOCK, LANES)
        edge = jnp.where(causal[None], edge, NEG).reshape(chunk, LANES)
        s = jnp.concatenate([edge, s[:, LANES:]], axis=1)
        top = jnp.max(s, axis=1, keepdims=True)
        weights[pair, half * chunk : (half + 1) * chunk, :] = jnp.exp2((s - top) * scale).astype(
            jnp.bfloat16
        )

    units = groups * blocks * 2

    def stage(n):
        if n % (2 * blocks) == 0 and n < units:
            near_keys(n // 2)
        if n < units:
            multiply(n)
        if n > 0:
            soften(n - 1)
        if n % 2 and (n + 1) % (2 * blocks):
            near_keys((n + 1) // 2)

    def attend(pair):
        group, b = divmod(pair, blocks)
        if b == 0:
            near_values(pair)
        if b + 1 < blocks:
            near_values(pair + 1)
        for half in range(2):
            o = jnp.dot(
                weights[pair, half * chunk : (half + 1) * chunk, :],
                near_rows[pair % 2],
                preferred_element_type=jnp.float32,
            )
            o = (o[:, 0:LANES] / o[:, LANES:]).astype(jnp.bfloat16)
            for h in range(half_heads):
                column = (group * heads_per + half * half_heads + h) * D_VALUE
                out_ref[b * BLOCK : (b + 1) * BLOCK, column : column + D_VALUE] = o[
                    h * BLOCK : (h + 1) * BLOCK
                ]

    def send_own(j):
        all_copies[j] = copies_of(
            1 + j % 2, peers, rows, tables[j], send_sem.at[j], recv_sem.at[j]
        )
        loads[2 * j].wait()
        loads[2 * j + 1].wait()
        go(j, range(0, 4))

    counts[0] = jnp.ones((BLOCK, LANES), jnp.bfloat16)
    counts[1] = jnp.zeros((BLOCK, LANES), jnp.bfloat16)
    place_copies = [
        pltpu.make_async_copy(place_stage, place_ref, place_sem.at[0]),
        pltpu.make_async_copy(count_stage, count_ref, place_sem.at[1]),
    ]
    steps = {
        "0": send_own,
        "1": step1,
        "2": step2,
        "3": step3,
        "4": step4,
        "5": step5,
        "q": prepare,
        "s": stage,
        "v": attend,
    }
    for step in PLAN:
        if step == "s0":
            for copy in place_copies:
                copy.wait()
        steps[step[0]](int(step[1:]))
        if step in SENT:
            for copy in all_copies[SENT.index(step)]:
                copy.wait_send()
        if step == "q0":
            sel_load.wait()
            place_stage[...], count_stage[...] = places_of(sel_stage[...], first_block)
        if step == "q1":
            for copy in place_copies:
                copy.start()


def per_device(queries, keys, values, selected):
    rows = queries.shape[0]
    blocks = rows // BLOCK
    groups = keys.shape[1] // D_HEAD
    heads_per = queries.shape[1] // (groups * D_HEAD)
    entries = blocks * 2 * SIDE * SIDE + 1
    spots = selected.shape[2] * BLOCK
    anywhere = pl.BlockSpec(memory_space=pl.ANY)
    return pl.pallas_call(
        functools.partial(kernel, heads_per),
        out_shape=pltpu.VMEM((rows, groups * heads_per * D_VALUE), jnp.bfloat16),
        in_specs=[anywhere, anywhere, anywhere, anywhere],
        out_specs=pl.BlockSpec(memory_space=pltpu.VMEM),
        scratch_shapes=[pltpu.VMEM((entries, BLOCK, LANES), jnp.bfloat16)] * 5
        + [pltpu.VMEM((heads_per // 2 * BLOCK, spots), jnp.float32)] * 2
        + [
            pltpu.VMEM((groups * blocks, heads_per * BLOCK, spots), jnp.bfloat16),
            pltpu.VMEM((2, spots, 2 * LANES), jnp.bfloat16),
            pltpu.VMEM((2, BLOCK, LANES), jnp.bfloat16),
            pltpu.VMEM(selected.shape, jnp.int32),
            pltpu.VMEM(selected.shape, jnp.int32),
            pltpu.VMEM(selected.shape, jnp.int32),
            pltpu.SMEM(selected.shape, jnp.int32),
            pltpu.SMEM(selected.shape, jnp.int32),
            pltpu.SemaphoreType.DMA((5, PIECES)),
            pltpu.SemaphoreType.DMA((5, PIECES)),
            pltpu.SemaphoreType.DMA((10,)),
            pltpu.SemaphoreType.DMA((blocks, groups * heads_per // 4)),
            pltpu.SemaphoreType.DMA((3,)),
        ],
        compiler_params=pltpu.CompilerParams(
            collective_id=0, has_side_effects=True, vmem_limit_bytes=60 * 1000 * 1000
        ),
        name="gather_attend",
    )(
        selected,
        queries,
        keys.reshape(blocks, BLOCK, keys.shape[1]),
        values.reshape(blocks, BLOCK, values.shape[1]),
    )


def solution(mesh):
    rows = P(("batch", "ctx"), None)
    return jax.shard_map(
        per_device,
        mesh=mesh,
        in_specs=(rows, rows, rows, P(("batch", "ctx"), None, None)),
        out_specs=rows,
        check_vma=False,
    )
```

time: 71.4 us -> 61.5 us (0.86)
  Pallas kernels: 67.3 us -> 59.7 us
  local copies, waits for them, and re-layouts: 3.91 us -> 1.67 us
    pallas_call x1, Pallas kernels: 67.3 us -> 59.7 us  [per_device(): pl.pallas_call(functools.partial(kernel, heads_per), out_shape=pltpu.VMEM...]
    unnamed x1, local copies, waits for them, and re-layouts: 3.91 us -> 1.67 us
where the time goes in v2:
time: 61.5 us; the launch traced here: 61.4 us
  Pallas kernels  59.7 us (97%)
  local copies, waits for them, and re-layouts  1.67 us (3%)
    pallas_call x1, Pallas kernels, per_device(): pl.pallas_call(functools.partial(kernel, heads_per), out_shape=pltpu.VMEM...  59.7 us
    unnamed x1, local copies, waits for them, and re-layouts  1.67 us

profile of v2, /device:TPU:1, one launch (start us, length us, event | category | flops | bytes accessed | tf_op | source)
XLA Modules:
  0.0 61.4 jit_solution(3445978788644171782)
XLA Ops:
  0.0 59.7 %gather_attend.1 = bf16[384,4096]{1,0:T(8,128)(2,1)S(1)} custom-call(s32[6,2,16]{2,1,0:T(2,128)} %sel_ref.1, bf16[384,6144]{1,0:T(8,128)(2,1)} %q_hbm.1, bf16[6,64,384]{2,1,0:T(8,128)(2,1)} %bitcast.2, bf16[6,64,256]{2,1,0:T(8,128)(2,1)} %bitcast.3), custom_call_target="tpu_custom_call" | custom-call | tf_op jit(solution)/shard_map/gather_attend/pallas_call | solution.py:396
  59.7 1.7 %copy.6 = bf16[384,4096]{1,0:T(8,128)(2,1)} copy(bf16[384,4096]{1,0:T(8,128)(2,1)S(1)} %gather_attend.1) | data formatting | bytes 6291456

commit v3 on v2

--- a/solution.py
+++ b/solution.py
@@ -15,16 +15,17 @@
 LANES = 128
 SHARD = 3
 BUNDLE = SIDE * SHARD
-PIECES = 24
+PIECES = 28
 NEG = -1e30
 PLAN = (
-    "01", "00", "02", "q0", "03", "11", "10", "04", "12", "q1", "q2", "13", "21", "q3", "20", "q4", "q5", "22", "31",
-    "30", "14", "32", "23", "41", "40", "50", "51", "s0", "42", "s1", "24", "s2", "s3", "s4", "s5", "s6", "s7", "s8",
-    "33", "52", "s9", "s10", "s11", "s12", "s13", "s14", "s15", "s16", "34", "s17", "s18", "s19", "s20",
-    "43", "s21", "s22", "s23", "s24", "53", "v0", "v1", "44", "v2", "v3", "v4", "v5", "54", "v6", "v7", "v8", "v9",
-    "v10", "v11",
+    "01", "q0", "q1", "00", "02", "03", "11", "04", "10", "12", "13", "21", "71", "q2",
+    "20", "70", "q3", "q4", "31", "30", "22", "72", "q5", "41", "60", "14", "61", "40",
+    "32", "23", "73", "50", "51", "s0", "s1", "s2", "62", "s3", "s4", "s5", "s6", "24",
+    "42", "s7", "s8", "s9", "s10", "33", "74", "s11", "52", "s12", "s13", "s14", "s15", "s16",
+    "34", "63", "s17", "s18", "s19", "s20", "43", "s21", "s22", "s23", "64", "s24", "53", "v0",
+    "v1", "v2", "44", "v3", "v4", "v5", "54", "v6", "v7", "v8", "v9", "v10", "v11",
 )
-SENT = ("v0", "v1", "v2", "v3", "v10")
+SENT = ("s6", "s10", "s16", "s24", "v10")
 EMPTY = 2 * 2 * SIDE * SIDE * 3
 
 
@@ -84,10 +85,10 @@
         ("row_right", first, rest, "left"),
         ("column_up", 0, rest, "down"),
         ("column_down", rest, first, "up"),
-        ("row", 0, BUNDLE, "down"),
-        ("row", 0, BUNDLE, "up"),
-        ("column", 0, BUNDLE, "right"),
-        ("column", 0, BUNDLE, "left"),
+        ("row", 0, half, "down"),
+        ("row", half, half, "up"),
+        ("column", 0, half, "right"),
+        ("column", half, half, "left"),
         ("row", 0, BUNDLE, "partner"),
         ("column", 0, BUNDLE, "partner"),
         ("row_up", 0, half, "down"),
@@ -100,6 +101,10 @@
         ("column_right", 0, BUNDLE, "partner"),
         ("row_far", 0, BUNDLE, "partner"),
         ("column_far", 0, BUNDLE, "partner"),
+        ("row", half, half, "down"),
+        ("row", 0, half, "up"),
+        ("column", half, half, "right"),
+        ("column", 0, half, "left"),
     ]
     made = []
     for n, (name, skip, count, peer) in enumerate(plan):
@@ -231,9 +236,16 @@
         arrived(j, range(4, 8))
         go(j, range(8, 14))
 
+    def step7(j):
+        go(j, range(24, 28))
+
     def step3(j):
         arrived(j, range(8, 12))
-        go(j, range(14, 22))
+        go(j, range(14, 18))
+
+    def step6(j):
+        arrived(j, range(24, 28))
+        go(j, range(18, 22))
 
     def step4(j):
         arrived(j, range(14, 18))
@@ -365,6 +377,8 @@
         "3": step3,
         "4": step4,
         "5": step5,
+        "6": step6,
+        "7": step7,
         "q": prepare,
         "s": stage,
         "v": attend,

time: 61.5 us -> 59.6 us (0.969)
  Pallas kernels: 59.7 us -> 57.9 us
    pallas_call x1, Pallas kernels: 59.7 us -> 57.9 us  [per_device(): pl.pallas_call(functools.partial(kernel, heads_per), out_shape=pltpu.VMEM...]
where the time goes in v3:
time: 59.6 us; the launch traced here: 59.5 us
  Pallas kernels  57.9 us (97%)
  local copies, waits for them, and re-layouts  1.67 us (3%)
    pallas_call x1, Pallas kernels, per_device(): pl.pallas_call(functools.partial(kernel, heads_per), out_shape=pltpu.VMEM...  57.9 us
    unnamed x1, local copies, waits for them, and re-layouts  1.67 us

profile of v3, /device:TPU:1, one launch (start us, length us, event | category | flops | bytes accessed | tf_op | source)
XLA Modules:
  0.0 59.5 jit_solution(2361315352592428577)
XLA Ops:
  0.0 57.9 %gather_attend.1 = bf16[384,4096]{1,0:T(8,128)(2,1)S(1)} custom-call(s32[6,2,16]{2,1,0:T(2,128)} %sel_ref.1, bf16[384,6144]{1,0:T(8,128)(2,1)} %q_hbm.1, bf16[6,64,384]{2,1,0:T(8,128)(2,1)} %bitcast.2, bf16[6,64,256]{2,1,0:T(8,128)(2,1)} %bitcast.3), custom_call_target="tpu_custom_call" | custom-call | tf_op jit(solution)/shard_map/gather_attend/pallas_call | solution.py:410
  57.9 1.7 %copy.6 = bf16[384,4096]{1,0:T(8,128)(2,1)} copy(bf16[384,4096]{1,0:T(8,128)(2,1)S(1)} %gather_attend.1) | data formatting | bytes 6291456
